TPU v7x, 32 devices: a whole 2x2x4 slice. The times are simulated.
32 devices in a mesh: dp: 8 (over z, y), expert: 2 (over core), tensor: 2 (over x).
Axes of the slice: x: 2, y: 2, z: 4, core: 2. Of those that a mesh axis runs over, the one named last changes fastest.
Arguments:
- dense_act: bfloat16 [2, 32, 512, 3584], P(None, 'dp', 'expert', 'tensor'), may hold values from -6 to 6
- dense_cot: bfloat16 [2, 32, 512, 3584], P(None, 'dp', ('expert', 'tensor')), may hold values from -6 to 6
- dense_proj_in: bfloat16 [2, 3584, 128], P(None, 'tensor'), may hold values from -0.09375 to 0.09375
- dense_proj_out: bfloat16 [2, 3584, 128], replicated, may hold values from -0.09375 to 0.09375
- expert_act: bfloat16 [32, 8, 64, 2560], P('dp', 'expert', None, 'tensor'), may hold values from -6 to 6
- expert_cot: bfloat16 [32, 8, 64, 3584], P('dp', 'expert', 'tensor'), may hold values from -6 to 6
- expert_proj_in: bfloat16 [2560, 128], P('tensor'), may hold values from -0.125 to 0.125
- expert_proj_out: bfloat16 [3584, 128], replicated, may hold values from -0.09375 to 0.09375
- dense_valid: float32 [2, 128, 128], replicated, may hold values from -0.0012207031 to 0.0012207031
- expert_valid: float32 [8, 128, 128], P('expert'), may hold values from -0.0012207031 to 0.0012207031
- domain_ids: int32 [32], P('dp'), may hold values from 0 to 63
- prior_mix: float32 [64], replicated, may hold values from 0.002 to 0.05
Outputs:
- log_mixture_weights: float32 [64], P('dp')
All inputs are finite; a program needn't handle non-finite values.
Results may differ from a plain program's by a relative error of at most 0.0003.
Values sent between devices are 32-bit elements; how exact they have to be, the bound alone decides.
A program may use at most 128 MiB of HBM per device.

v0:
```python
import jax
import jax.numpy as jnp
from jax import lax
from jax.sharding import PartitionSpec as P


def per_device(
    dense_act,
    dense_cot,
    dense_proj_in,
    dense_proj_out,
    expert_act,
    expert_cot,
    expert_proj_in,
    expert_proj_out,
    dense_valid,
    expert_valid,
    domain_ids,
    prior_mix,
):
    block = dense_act
    dense_update_vector = lax.psum_scatter(
        jnp.einsum("lmtd,ldr->tlmr", block, dense_proj_in, preferred_element_type=jnp.float32),
        "tensor",
        scatter_dimension=0,
        tiled=True,
    )
    dense_weight_matrix = jnp.einsum(
        "lmtd,ldr->tlmr", dense_cot, dense_proj_out, preferred_element_type=jnp.float32
    )
    dense_portion = jnp.einsum(
        "fquy,fquh->quyh", dense_update_vector, dense_weight_matrix, precision=lax.Precision.HIGHEST
    )
    block = expert_act
    expert_u = lax.psum_scatter(
        jnp.einsum("mecf,fr->cmer", block, expert_proj_in, preferred_element_type=jnp.float32),
        "tensor",
        scatter_dimension=0,
        tiled=True,
    )
    expert_weight_matrix = jnp.einsum(
        "mecd,dr->cmer", expert_cot, expert_proj_out, preferred_element_type=jnp.float32
    )
    expert_part = jnp.einsum(
        "cmer,cmes->mers", expert_u, expert_weight_matrix, precision=lax.Precision.HIGHEST
    )
    dense_full = lax.psum(dense_portion, ("expert", "tensor"))
    dense_score = jnp.sum(dense_full * dense_valid[:, None], axis=(0, 2, 3))
    expert_full = lax.psum(expert_part, "tensor")
    expert_local = jnp.sum(expert_full * expert_valid[None], axis=(1, 2, 3))
    score = dense_score + lax.psum(expert_local, "expert")
    domains = prior_mix.shape[0]
    onehot = (domain_ids[:, None] == jnp.arange(domains, dtype=jnp.int32)[None, :]).astype(
        jnp.float32
    )
    domain_part = jnp.dot(score, onehot, precision=lax.Precision.HIGHEST)
    share_tally_count = domains // lax.axis_size("dp")
    first_domain = lax.axis_index("dp") * share_tally_count
    previous_domain_share = lax.dynamic_slice_in_dim(prior_mix, first_domain, share_tally_count, 0)
    domain_total = lax.psum(domain_part, "dp")
    spread = jnp.sqrt(jnp.mean(domain_total * domain_total) + 1e-06)
    z_value = domain_total / spread
    mass = jnp.sum(prior_mix * jnp.exp(0.5 * z_value))
    z_share = lax.dynamic_slice_in_dim(z_value, first_domain, share_tally_count, 0)
    return jnp.log(previous_domain_share) + 0.5 * z_share - jnp.log(mass)


def solution(mesh):
    placed = (
        P(None, "dp", "expert", "tensor"),
        P(None, "dp", ("expert", "tensor"), None),
        P(None, "tensor", None),
        P(),
        P("dp", "expert", None, "tensor"),
        P("dp", "expert", "tensor", None),
        P("tensor", None),
        P(),
        P(),
        P("expert", None, None),
        P("dp"),
        P(),
    )
    return jax.shard_map(per_device, mesh=mesh, in_specs=placed, out_specs=P("dp"), check_vma=False)
```

profile of v0, /device:TPU:0, one launch (start us, length us, event | category | flops | bytes accessed | tf_op | source)
XLA Modules:
  0.0 206.4 jit_solution(693878961875852554)
XLA Ops:
  6.5 0.0 copy-start
  6.5 0.0 copy-start.3
  6.5 0.0 all-reduce.9.cloned.1.call-start
  6.5 1.7 copy-done
  8.3 1.8 convolution_bitcast_fusion.1
  10.1 1.1 copy.18
  11.2 0.0 all-reduce.9.cloned.1.call-update
  11.3 0.0 reduce-scatter.4.cloned.1.call-start
  11.3 0.0 copy-done.3
  11.3 5.6 %convolution_bitcast_fusion = f32[256,2,4,128]{0,3,2,1:T(8,128)S(1)} fusion(bf16[2,4,256,1792]{3,2,1,0:T(8,128)(2,1)} %param.12, bf16[2,1792,128]{2,1,0:T(8,128)(2,1)S(1)} %copy-done.3), kind=kOutput, calls=%fused_computation.2 | convolution fusion | flops 939524096 | bytes 9306112 | tf_op jit(solution)/shard_map/lmtd,ldr->tlmr/dot_general | solution.py:23
  16.9 26.2 %copy.29 = f32[256,2,4,128]{2,3,1,0:T(8,128)} copy(f32[256,2,4,128]{0,3,2,1:T(8,128)S(1)} %convolution_bitcast_fusion) | data formatting | bytes 2097152
  43.2 0.0 copy-start.9
  43.2 0.0 copy-start.7
  43.2 29.4 %reshape.9 = f32[256,1024]{1,0:T(8,128)} reshape(f32[256,2,128,4]{3,2,1,0:T(8,128)} %bitcast.46) | data formatting | bytes 2097152
  72.5 0.0 reduce-scatter.4.cloned.1.call-update
  72.6 0.0 all-reduce.7.cloned.1.call-start
  72.6 0.0 copy-done.9
  72.6 0.6 dynamic-slice
  73.9 0.0 copy-done.7
  73.9 0.0 copy-start.2
  73.9 3.3 %fusion.6 = f32[128,4,4,32]{0,3,2,1:T(8,128)S(1)} fusion(bf16[4,4,32,3584]{3,2,1,0:T(8,128)(2,1)} %param.17, bf16[3584,128]{1,0:T(8,128)(2,1)S(1)} %copy-done.7), kind=kOutput, calls=%fused_computation.8 | convolution fusion | flops 469762048 | bytes 4849664 | tf_op jit(solution)/shard_map/mecd,dr->cmer/dot_general | solution.py:41
  77.2 0.0 all-reduce.9.cloned.1.call-done
  77.2 1.0 constant_dynamic-slice_fusion
  78.2 2.8 %fusion.9 = f32[4,4,128,128]{3,2,1,0:T(8,128)} fusion(f32[128,4,4,32]{0,3,2,1:T(8,128)S(1)} %fusion.6, f32[32,4,4,128]{3,2,1,0:T(4,128)S(1)} %constant_dynamic-slice_fusion), kind=kOutput, calls=%fused_computation.12 | convolution fusion | flops 100663296 | bytes 1572864 | tf_op jit(solution)/shard_map/cmer,cmes->mers/dot_general | solution.py:44
  81.0 0.0 all-reduce.7.cloned.1.call-update
  81.0 0.2 all-reduce.5.cloned.1.call-start
  81.3 0.0 copy-done.2
  81.3 5.6 %fusion.2 = f32[128,2,4,128]{0,3,2,1:T(8,128)S(1)} fusion(bf16[2,4,128,3584]{3,2,1,0:T(8,128)(2,1)} %param.13, bf16[2,3584,128]{2,1,0:T(8,128)(2,1)S(1)} %copy-done.2), kind=kOutput, calls=%fused_computation.3 | convolution fusion | flops 939524096 | bytes 9699328 | tf_op jit(solution)/shard_map/lmtd,ldr->tlmr/dot_general | solution.py:28
  86.9 8.9 %reduce-scatter.4.cloned.1.call-done = f32[128,1024]{1,0:T(8,128)} async-done(((f32[256,1024]{1,0:T(8,128)}), f32[128,1024]{1,0:T(8,128)}) %reduce-scatter.4.cloned.1.call-update) | async-done | bytes 524304
  95.8 19.5 %reshape.10 = f32[128,2,128,4]{3,2,1,0:T(8,128)} reshape(f32[128,1024]{1,0:T(8,128)} %reduce-scatter.4.cloned.1.call-done) | data formatting | bytes 1048576
  115.3 13.2 %copy.16 = f32[128,2,4,128]{0,3,2,1:T(8,128)} copy(f32[128,2,4,128]{2,3,1,0:T(8,128)} %bitcast.47) | data formatting | bytes 1048576 | tf_op jit(solution)/shard_map/reduce_scatter | solution.py:22
  128.5 3.1 %fusion.12 = f32[2,4,128,128]{3,2,1,0:T(8,128)} fusion(f32[128,2,4,128]{0,3,2,1:T(8,128)} %copy.16, f32[128,2,4,128]{0,3,2,1:T(8,128)S(1)} %fusion.2), kind=kOutput, calls=%fused_computation.22 | convolution fusion | flops 201326592 | bytes 1572864 | tf_op jit(solution)/shard_map/fquy,fquh->quyh/dot_general | solution.py:31
  131.6 0.0 all-reduce.5.cloned.1.call-update
  131.6 6.7 %all-reduce.7.cloned.1.call-done = f32[4,4,128,128]{3,2,1,0:T(8,128)} async-done(((f32[4,4,128,128]{3,2,1,0:T(8,128)}), f32[4,4,128,128]{3,2,1,0:T(8,128)}) %all-reduce.7.cloned.1.call-update) | async-done | bytes 1048592 | tf_op jit(solution)/shard_map/psum | solution.py:49
  138.3 0.0 copy-done.4
  138.3 1.4 multiply_reduce_fusion
  139.7 2.4 %psum.30 = f32[4]{0:T(128)S(1)} all-reduce(f32[4]{0:T(128)S(1)} %multiply_reduce_fusion), channel_id=1, replica_groups=mesh['dp'=8,'expert'=2,'tensor'=2] {'expert'}, use_global_device_ids=true, to_apply=%region_6.0 | all-reduce | flops 4 | bytes 32 | tf_op jit(solution)/shard_map/psum | solution.py:51
  142.1 31.8 %all-reduce.5.cloned.1.call-done = f32[2,4,128,128]{3,2,1,0:T(8,128)} async-done(((f32[2,4,128,128]{3,2,1,0:T(8,128)}), f32[2,4,128,128]{3,2,1,0:T(8,128)}) %all-reduce.5.cloned.1.call-update) | async-done | bytes 524304 | tf_op jit(solution)/shard_map/psum | solution.py:47
  173.9 0.0 copy-done.5
  173.9 1.2 multiply_reduce_fusion.1
  175.1 0.0 copy-done.8
  175.1 0.2 convolution_bitcast_fusion.2
  175.3 21.3 %psum.31 = f32[64]{0:T(128)S(1)} all-reduce(f32[64]{0:T(128)S(1)} %convolution_bitcast_fusion.2), channel_id=1, replica_groups=mesh['dp'=8,'expert'=2,'tensor'=2] {'dp'}, use_global_device_ids=true, to_apply=%region_7.0 | all-reduce | flops 64 | bytes 512 | tf_op jit(solution)/shard_map/psum | solution.py:60
  196.7 0.6 multiply_reduce_fusion.3
  198.0 0.0 copy-done.6
  198.0 0.6 multiply_reduce_fusion.2
  199.3 0.6 add_subtract_fusion
  199.9 0.0 copy-done.1
  (5 shorter events, 0.0 us)
Async XLA Ops:
  6.5 1.7 copy-start
  6.5 4.8 %copy-start.3 = (bf16[2,1792,128]{2,1,0:T(8,128)(2,1)S(1)}, bf16[2,1792,128]{2,1,0:T(8,128)(2,1)}, u32[]{:S(2)}) copy-start(bf16[2,1792,128]{2,1,0:T(8,128)(2,1)} %param.14) | copy-start | bytes 2752516
  6.5 70.6 %all-reduce.9.cloned.1.call-start = ((), (), s32[]{:S(2)}) async-start(), calls=%async_computation.4 | async-start | bytes 1048576
  11.3 84.6 %reduce-scatter.4.cloned.1.call-start = ((), (), s32[]{:S(2)}) async-start(), calls=%async_computation.3 | async-start | bytes 1572864
  43.2 29.4 %copy-start.9 = (u32[32]{0:T(128)S(1)}, u32[32]{0:T(128)}, u32[]{:S(2)}) copy-start(u32[32]{0:T(128)} %constant.29) | copy-start | bytes 388
  43.2 30.7 %copy-start.7 = (bf16[3584,128]{1,0:T(8,128)(2,1)S(1)}, bf16[3584,128]{1,0:T(8,128)(2,1)}, u32[]{:S(2)}) copy-start(bf16[3584,128]{1,0:T(8,128)(2,1)} %param.19) | copy-start | bytes 2752516
  72.6 65.7 %all-reduce.7.cloned.1.call-start = ((), (), s32[]{:S(2)}) async-start(), calls=%async_computation.2 | async-start | bytes 2097152 | tf_op jit(solution)/shard_map/psum | solution.py:49
  73.9 7.4 %copy-start.2 = (bf16[2,3584,128]{2,1,0:T(8,128)(2,1)S(1)}, bf16[2,3584,128]{2,1,0:T(8,128)(2,1)}, u32[]{:S(2)}) copy-start(bf16[2,3584,128]{2,1,0:T(8,128)(2,1)} %param.15) | copy-start | bytes 5505028
  81.0 92.9 %all-reduce.5.cloned.1.call-start = ((), (), s32[]{:S(2)}) async-start(), calls=%async_computation.1 | async-start | bytes 1048576 | tf_op jit(solution)/shard_map/psum | solution.py:47
  115.3 22.9 %copy-start.4 = (f32[4,128,128]{2,1,0:T(8,128)S(1)}, f32[4,128,128]{2,1,0:T(8,128)}, u32[]{:S(2)}) copy-start(f32[4,128,128]{2,1,0:T(8,128)} %param.21) | copy-start | bytes 786436
  115.3 58.6 %copy-start.5 = (f32[2,128,128]{2,1,0:T(8,128)S(1)}, f32[2,128,128]{2,1,0:T(8,128)}, u32[]{:S(2)}) copy-start(f32[2,128,128]{2,1,0:T(8,128)} %param.20) | copy-start | bytes 393220
  115.3 84.5 %copy-start.1 = (bf16[4,4,64,1280]{3,2,1,0:T(8,128)(2,1)S(1)}, bf16[4,4,64,1280]{3,2,1,0:T(8,128)(2,1)}, u32[]{:S(2)}) copy-start(bf16[4,4,64,1280]{3,2,1,0:T(8,128)(2,1)} %param.16) | copy-start | bytes 7864324
  128.5 46.6 %copy-start.8 = (s32[4]{0:T(128)S(1)}, s32[4]{0:T(128)}, u32[]{:S(2)}) copy-start(s32[4]{0:T(128)} %param.22) | copy-start | bytes 52
  128.5 69.5 %copy-start.6 = (f32[64]{0:T(128)S(1)}, f32[64]{0:T(128)}, u32[]{:S(2)}) copy-start(f32[64]{0:T(128)} %param.23) | copy-start | bytes 772
Sparse Core Ops, SparseCore 0:
  11.4 31.3 all-reduce.8
  72.7 23.1 reduce-scatter.3
  98.1 40.0 all-reduce.6
  140.5 33.4 all-reduce.4
where the time goes:
time: 207 us; the launch traced here: 206 us
  local copies, waits for them, and re-layouts  92.7 us (45%)
  waiting for transfers between devices  47.4 us (23%)
  blocking collectives  23.8 us (11%)
  matrix products  22.5 us (11%)
  between operations  15.3 us (7%)
  other arithmetic  4.44 us (2%)
    unnamed x25, local copies, waits for them, and re-layouts  78.4 us
    psum x1, waiting for transfers between devices, per_device(): dense_full = lax.psum(dense_portion, ('expert', 'tensor'))  31.8 us
    psum x1, blocking collectives, per_device(): domain_total = lax.psum(domain_part, 'dp')  21.3 us
    reduce_scatter x1, local copies, waits for them, and re-layouts, per_device(): lax.psum_scatter(jnp.einsum('lmtd,ldr->tlmr', block, dense_proj_in, prefe...  13.2 us
    unnamed x6, waiting for transfers between devices  8.98 us
    psum x1, waiting for transfers between devices, per_device(): expert_full = lax.psum(expert_part, 'tensor')  6.66 us
    dot_general x1, matrix products, per_device(): jnp.einsum('lmtd,ldr->tlmr', dense_cot, dense_proj_out, preferred_element...  5.64 us
    dot_general x1, matrix products, per_device(): jnp.einsum('lmtd,ldr->tlmr', block, dense_proj_in, preferred_element_type...  5.62 us
  transfers between devices with their start and end apart: 4, of which 3 were waited for; matrix products, arithmetic and copies ran while one was open for 54% of the time, Pallas kernels for 0%

commit v1 on v0

--- a/solution.py
+++ b/solution.py
@@ -44,7 +44,7 @@
     expert_part = jnp.einsum(
         "cmer,cmes->mers", expert_u, expert_weight_matrix, precision=lax.Precision.HIGHEST
     )
-    dense_full = lax.psum(dense_portion, ("expert", "tensor"))
+    dense_full = lax.psum(lax.psum(dense_portion, "tensor"), "expert")
     dense_score = jnp.sum(dense_full * dense_valid[:, None], axis=(0, 2, 3))
     expert_full = lax.psum(expert_part, "tensor")
     expert_local = jnp.sum(expert_full * expert_valid[None], axis=(1, 2, 3))

time: 207 us -> 237 us (1.14)
  waiting for transfers between devices: 47.4 us -> 77.8 us
    psum x2, waiting for transfers between devices: 38.4 us -> 68.6 us  [per_device(): dense_full = lax.psum(lax.psum(dense_portion, 'tensor'), 'expert')]
  transfers between devices with their start and end apart: 4 -> 4, of which waited for: 3 -> 3; matrix products, arithmetic and copies ran while one was open for 54% -> 32% of each run, Pallas kernels for 0% -> 0%
where the time goes in v1:
time: 237 us
  local copies, waits for them, and re-layouts  92.5 us (39%)
  waiting for transfers between devices  77.8 us (33%)
  blocking collectives  24.1 us (10%)
  matrix products  22.3 us (9%)
  between operations  15.3 us (6%)
  other arithmetic  4.44 us (2%)
    unnamed x25, local copies, waits for them, and re-layouts  78.4 us
    psum x2, waiting for transfers between devices, per_device(): dense_full = lax.psum(lax.psum(dense_portion, 'tensor'), 'expert')  68.6 us
    psum x1, blocking collectives, per_device(): domain_total = lax.psum(domain_part, 'dp')  21.6 us
    reduce_scatter x1, local copies, waits for them, and re-layouts, per_device(): lax.psum_scatter(jnp.einsum('lmtd,ldr->tlmr', block, dense_proj_in, prefe...  13 us
    unnamed x6, waiting for transfers between devices  9.25 us
    dot_general x1, matrix products, per_device(): jnp.einsum('lmtd,ldr->tlmr', dense_cot, dense_proj_out, preferred_element...  5.62 us
    dot_general x1, matrix products, per_device(): jnp.einsum('lmtd,ldr->tlmr', block, dense_proj_in, preferred_element_type...  5.62 us
  transfers between devices with their start and end apart: 4, of which 3 were waited for; matrix products, arithmetic and copies ran while one was open for 32% of the time, Pallas kernels for 0%

profile of v1, /device:TPU:0, one launch (start us, length us, event | category | flops | bytes accessed | tf_op | source)
XLA Modules:
  0.0 236.8 jit_solution(13737868965483552507)
XLA Ops:
  6.5 0.0 copy-start
  6.5 0.0 copy-start.3
  6.5 0.0 all-reduce.8.cloned.1.call-start
  6.5 1.7 copy-done
  8.3 1.8 convolution_bitcast_fusion.1
  10.1 1.1 copy.18
  11.2 0.0 all-reduce.8.cloned.1.call-update
  11.3 0.0 reduce-scatter.4.cloned.1.call-start
  11.3 0.0 copy-done.3
  11.3 5.6 %convolution_bitcast_fusion = f32[256,2,4,128]{0,3,2,1:T(8,128)S(1)} fusion(bf16[2,4,256,1792]{3,2,1,0:T(8,128)(2,1)} %param.12, bf16[2,1792,128]{2,1,0:T(8,128)(2,1)S(1)} %copy-done.3), kind=kOutput, calls=%fused_computation.2 | convolution fusion | flops 939524096 | bytes 9306112 | tf_op jit(solution)/shard_map/lmtd,ldr->tlmr/dot_general | solution.py:23
  16.9 26.2 %copy.29 = f32[256,2,4,128]{2,3,1,0:T(8,128)} copy(f32[256,2,4,128]{0,3,2,1:T(8,128)S(1)} %convolution_bitcast_fusion) | data formatting | bytes 2097152
  43.2 0.0 copy-start.9
  43.2 0.0 copy-start.7
  43.2 29.4 %reshape.9 = f32[256,1024]{1,0:T(8,128)} reshape(f32[256,2,128,4]{3,2,1,0:T(8,128)} %bitcast.46) | data formatting | bytes 2097152
  72.5 0.0 reduce-scatter.4.cloned.1.call-update
  72.6 0.0 copy-start.2
  72.6 0.2 all-reduce.10.cloned.1.call-start
  72.8 0.0 copy-done.9
  72.8 0.6 dynamic-slice
  74.0 0.0 copy-done.7
  74.1 3.2 %fusion.6 = f32[128,4,4,32]{0,3,2,1:T(8,128)S(1)} fusion(bf16[4,4,32,3584]{3,2,1,0:T(8,128)(2,1)} %param.17, bf16[3584,128]{1,0:T(8,128)(2,1)S(1)} %copy-done.7), kind=kOutput, calls=%fused_computation.8 | convolution fusion | flops 469762048 | bytes 4849664 | tf_op jit(solution)/shard_map/mecd,dr->cmer/dot_general | solution.py:41
  77.2 0.0 copy-done.2
  77.2 5.6 %fusion.2 = f32[128,2,4,128]{0,3,2,1:T(8,128)S(1)} fusion(bf16[2,4,128,3584]{3,2,1,0:T(8,128)(2,1)} %param.13, bf16[2,3584,128]{2,1,0:T(8,128)(2,1)S(1)} %copy-done.2), kind=kOutput, calls=%fused_computation.3 | convolution fusion | flops 939524096 | bytes 9699328 | tf_op jit(solution)/shard_map/lmtd,ldr->tlmr/dot_general | solution.py:28
  82.9 0.0 all-reduce.8.cloned.1.call-done
  82.9 1.0 constant_dynamic-slice_fusion
  83.9 2.8 %fusion.9 = f32[4,4,128,128]{3,2,1,0:T(8,128)} fusion(f32[128,4,4,32]{0,3,2,1:T(8,128)S(1)} %fusion.6, f32[32,4,4,128]{3,2,1,0:T(4,128)S(1)} %constant_dynamic-slice_fusion), kind=kOutput, calls=%fused_computation.12 | convolution fusion | flops 100663296 | bytes 1572864 | tf_op jit(solution)/shard_map/cmer,cmes->mers/dot_general | solution.py:44
  86.7 9.2 %reduce-scatter.4.cloned.1.call-done = f32[128,1024]{1,0:T(8,128)} async-done(((f32[256,1024]{1,0:T(8,128)}), f32[128,1024]{1,0:T(8,128)}) %reduce-scatter.4.cloned.1.call-update) | async-done | bytes 524304
  95.8 19.5 %reshape.10 = f32[128,2,128,4]{3,2,1,0:T(8,128)} reshape(f32[128,1024]{1,0:T(8,128)} %reduce-scatter.4.cloned.1.call-done) | data formatting | bytes 1048576
  115.3 13.0 %copy.16 = f32[128,2,4,128]{0,3,2,1:T(8,128)} copy(f32[128,2,4,128]{2,3,1,0:T(8,128)} %bitcast.47) | data formatting | bytes 1048576 | tf_op jit(solution)/shard_map/reduce_scatter | solution.py:22
  128.4 3.1 %fusion.12 = f32[2,4,128,128]{3,2,1,0:T(8,128)} fusion(f32[128,2,4,128]{0,3,2,1:T(8,128)} %copy.16, f32[128,2,4,128]{0,3,2,1:T(8,128)S(1)} %fusion.2), kind=kOutput, calls=%fused_computation.22 | convolution fusion | flops 201326592 | bytes 1572864 | tf_op jit(solution)/shard_map/fquy,fquh->quyh/dot_general | solution.py:31
  131.5 0.0 all-reduce.10.cloned.1.call-update
  131.5 0.0 all-reduce.6.cloned.1.call-start
  131.5 51.7 %all-reduce.10.cloned.1.call-done = (f32[2,4,128,128]{3,2,1,0:T(8,128)}, f32[4,4,128,128]{3,2,1,0:T(8,128)}) async-done(((f32[2,4,128,128]{3,2,1,0:T(8,128)}, f32[4,4,128,128]{3,2,1,0:T(8,128)}), (f32[2,4,128,128]{3,2,1,0:T(8,128)}, f32[4,4,128,128]{3,2,1,0:T(8,128)})) %all-reduce.10.cloned.1.call-update) | async-done | bytes 1572880 | tf_op jit(solution)/shard_map/psum | solution.py:47
  183.2 0.0 all-reduce.6.cloned.1.call-update
  183.2 0.0 copy-done.4
  183.2 1.4 multiply_reduce_fusion
  184.7 2.4 %psum.38 = f32[4]{0:T(128)S(1)} all-reduce(f32[4]{0:T(128)S(1)} %multiply_reduce_fusion), channel_id=1, replica_groups=mesh['dp'=8,'expert'=2,'tensor'=2] {'expert'}, use_global_device_ids=true, to_apply=%region_7.0 | all-reduce | flops 4 | bytes 32 | tf_op jit(solution)/shard_map/psum | solution.py:51
  187.1 16.9 %all-reduce.6.cloned.1.call-done = f32[2,4,128,128]{3,2,1,0:T(8,128)} async-done(((f32[2,4,128,128]{3,2,1,0:T(8,128)}), f32[2,4,128,128]{3,2,1,0:T(8,128)}) %all-reduce.6.cloned.1.call-update) | async-done | bytes 524304 | tf_op jit(solution)/shard_map/psum | solution.py:47
  204.0 0.0 copy-done.5
  204.0 1.2 multiply_reduce_fusion.1
  205.2 0.0 copy-done.8
  205.2 0.2 convolution_bitcast_fusion.2
  205.4 21.6 %psum.39 = f32[64]{0:T(128)S(1)} all-reduce(f32[64]{0:T(128)S(1)} %convolution_bitcast_fusion.2), channel_id=1, replica_groups=mesh['dp'=8,'expert'=2,'tensor'=2] {'dp'}, use_global_device_ids=true, to_apply=%region_8.0 | all-reduce | flops 64 | bytes 512 | tf_op jit(solution)/shard_map/psum | solution.py:60
  227.1 0.6 multiply_reduce_fusion.3
  228.4 0.0 copy-done.6
  228.4 0.6 multiply_reduce_fusion.2
  229.7 0.6 add_subtract_fusion
  230.3 0.0 copy-done.1
  (5 shorter events, 0.0 us)
Async XLA Ops:
  6.5 1.7 copy-start
  6.5 4.8 %copy-start.3 = (bf16[2,1792,128]{2,1,0:T(8,128)(2,1)S(1)}, bf16[2,1792,128]{2,1,0:T(8,128)(2,1)}, u32[]{:S(2)}) copy-start(bf16[2,1792,128]{2,1,0:T(8,128)(2,1)} %param.14) | copy-start | bytes 2752516
  6.5 76.3 %all-reduce.8.cloned.1.call-start = ((), (), s32[]{:S(2)}) async-start(), calls=%async_computation.3 | async-start | bytes 1048576
  11.3 84.6 %reduce-scatter.4.cloned.1.call-start = ((), (), s32[]{:S(2)}) async-start(), calls=%async_computation.2 | async-start | bytes 1572864
  43.2 29.6 %copy-start.9 = (u32[32]{0:T(128)S(1)}, u32[32]{0:T(128)}, u32[]{:S(2)}) copy-start(u32[32]{0:T(128)} %constant.29) | copy-start | bytes 388
  43.2 30.9 %copy-start.7 = (bf16[3584,128]{1,0:T(8,128)(2,1)S(1)}, bf16[3584,128]{1,0:T(8,128)(2,1)}, u32[]{:S(2)}) copy-start(bf16[3584,128]{1,0:T(8,128)(2,1)} %param.19) | copy-start | bytes 2752516
  72.6 4.7 %copy-start.2 = (bf16[2,3584,128]{2,1,0:T(8,128)(2,1)S(1)}, bf16[2,3584,128]{2,1,0:T(8,128)(2,1)}, u32[]{:S(2)}) copy-start(bf16[2,3584,128]{2,1,0:T(8,128)(2,1)} %param.15) | copy-start | bytes 5505028
  72.6 110.6 %all-reduce.10.cloned.1.call-start = ((), (), s32[]{:S(2)}) async-start(), calls=%async_computation.4 | async-start | bytes 3145728 | tf_op jit(solution)/shard_map/psum | solution.py:47
  115.3 115.0 %copy-start.1 = (bf16[4,4,64,1280]{3,2,1,0:T(8,128)(2,1)S(1)}, bf16[4,4,64,1280]{3,2,1,0:T(8,128)(2,1)}, u32[]{:S(2)}) copy-start(bf16[4,4,64,1280]{3,2,1,0:T(8,128)(2,1)} %param.16) | copy-start | bytes 7864324
  128.3 54.9 %copy-start.4 = (f32[4,128,128]{2,1,0:T(8,128)S(1)}, f32[4,128,128]{2,1,0:T(8,128)}, u32[]{:S(2)}) copy-start(f32[4,128,128]{2,1,0:T(8,128)} %param.21) | copy-start | bytes 786436
  128.3 75.7 %copy-start.5 = (f32[2,128,128]{2,1,0:T(8,128)S(1)}, f32[2,128,128]{2,1,0:T(8,128)}, u32[]{:S(2)}) copy-start(f32[2,128,128]{2,1,0:T(8,128)} %param.20) | copy-start | bytes 393220
  128.3 76.9 %copy-start.8 = (s32[4]{0:T(128)S(1)}, s32[4]{0:T(128)}, u32[]{:S(2)}) copy-start(s32[4]{0:T(128)} %param.22) | copy-start | bytes 52
  128.3 100.0 %copy-start.6 = (f32[64]{0:T(128)S(1)}, f32[64]{0:T(128)}, u32[]{:S(2)}) copy-start(f32[64]{0:T(128)} %param.23) | copy-start | bytes 772
  131.5 72.6 %all-reduce.6.cloned.1.call-start = ((), (), s32[]{:S(2)}) async-start(), calls=%async_computation.1 | async-start | bytes 1048576 | tf_op jit(solution)/shard_map/psum | solution.py:47
Sparse Core Ops, SparseCore 0:
  11.4 31.3 all-reduce.7
  72.7 23.1 reduce-scatter.3
  131.6 51.5 all-reduce.9
  185.4 18.5 all-reduce.5
